TPU v7x, 256 devices: a whole 4x4x8 slice. The times are simulated.
256 devices in a mesh: row: 4 (over z_hi, core), col: 16 (over z_lo, y), layer: 4 (over x).
Axes of the slice: x: 4, y: 4, z: 8 (z_hi: 2, z_lo: 4; z = z_hi * 4 + z_lo), core: 2. Of those that a mesh axis runs over, the one named last changes fastest.
Arguments:
- amplitudes: float32 [2016, 73536], P('row', ('layer', 'col')), may hold values from -6 to 6
- integrals: float32 [73536, 768], P(('layer', 'col'), 'row'), may hold values from -0.0625 to 0.0625
- occ_energy: float32 [64], replicated, may hold values from -2 to -0.5
- vir_energy: float32 [384], replicated, may hold values from 0.2 to 3
Outputs:
- ladder: float32 [2016, 768], P('col', ('row', 'layer'))
- amplitude_step: float32 [2016, 768], P('col', ('row', 'layer'))
All inputs are finite; a program needn't handle non-finite values.
Results may differ from a plain program's by a relative error of at most 0.00007.
Values sent between devices are 32-bit elements; how exact they have to be, the bound alone decides.
A program may use at most 64 MiB of HBM per device.

v0:
```python
import jax
import jax.numpy as jnp
import numpy as np
from jax import lax
from jax.sharding import PartitionSpec as P


def in_blocks(array, dim, count):
    shape = array.shape
    parts = array.reshape(*shape[:dim], count, shape[dim] // count, *shape[dim + 1 :])
    return jnp.moveaxis(parts, dim, 0)


def summed_on_arrival(array, axis, dim):
    count = lax.axis_size(axis)
    parts = lax.all_to_all(in_blocks(array, dim, count), axis, 0, 0, tiled=True)
    return jnp.sum(parts, axis=0)


def lookup(indices, values_table):
    positions = jnp.arange(values_table.shape[0], dtype=jnp.int32)
    picked = jnp.where(indices[:, None] == positions[None, :], values_table[None, :], 0.0)
    return jnp.sum(picked, axis=1)


def owner_blocks(partial_sum):
    col_count = lax.axis_size("col")
    layer_count = lax.axis_size("layer")
    pair_rows = partial_sum.shape[0] // col_count
    slab_cols = partial_sum.shape[1] // layer_count
    blocks = partial_sum.reshape(col_count, pair_rows, layer_count, slab_cols)
    return blocks.transpose(0, 2, 1, 3).reshape(col_count * layer_count * pair_rows, slab_cols)


def shards(amplitudes, integrals, occ_energy, vir_energy):
    partial_rows = jnp.dot(
        amplitudes,
        lax.all_gather(integrals, "row", axis=1, tiled=True),
        precision=lax.Precision.HIGHEST,
        preferred_element_type=jnp.float32,
    )
    partial_sum = lax.all_to_all(partial_rows, "row", split_axis=1, concat_axis=0, tiled=True)
    ladder = summed_on_arrival(owner_blocks(partial_sum), ("col", "layer"), 0)
    pair_rows = ladder.shape[0]
    slab_cols = ladder.shape[1]
    occupied = occ_energy.shape[0]
    virtuals = vir_energy.shape[0]
    first_np, second_np = np.triu_indices(occupied, 1)
    ij_start = lax.axis_index("col") * pair_rows
    ab_start = (
        lax.axis_index("row") * lax.axis_size("layer") + lax.axis_index("layer")
    ) * slab_cols
    first_index = lax.dynamic_slice_in_dim(
        jnp.asarray(first_np, dtype=jnp.int32), ij_start, pair_rows
    )
    second_index = lax.dynamic_slice_in_dim(
        jnp.asarray(second_np, dtype=jnp.int32), ij_start, pair_rows
    )
    pair_sum = lookup(first_index, occ_energy) + lookup(second_index, occ_energy)
    ab_index = ab_start + jnp.arange(slab_cols, dtype=jnp.int32)
    vir_sum = lookup(ab_index // virtuals, vir_energy) + lookup(ab_index % virtuals, vir_energy)
    denominator = pair_sum[:, None] - vir_sum[None, :]
    return (ladder, ladder / denominator)


def solution(mesh):
    in_specs = (P("row", ("layer", "col")), P(("layer", "col"), "row"), P(), P())
    out_specs = (P("col", ("row", "layer")), P("col", ("row", "layer")))
    return jax.shard_map(shards, mesh=mesh, in_specs=in_specs, out_specs=out_specs, check_vma=False)
```

profile of v0, /device:TPU:64, one launch (start us, length us, event | category | flops | bytes accessed | tf_op | source)
XLA Modules:
  0.0 186.8 jit_solution(8743574905029735897)
XLA Ops:
  7.2 0.0 copy-start
  7.2 0.0 all-gather.2.cloned.1.call-start
  7.2 0.7 all-gather.2.cloned.1.call-update
  7.9 61.1 %all-gather.2.cloned.1.call-done = f32[1149,768]{0,1:T(8,128)} async-done(((f32[1149,192]{0,1:T(8,128)}), f32[1149,768]{0,1:T(8,128)}) %all-gather.2.cloned.1.call-update) | async-done | bytes 3529744 | tf_op jit(solution)/shard_map/all_gather | solution.py:38
  69.0 0.0 copy-done
  69.0 8.3 %fusion.1 = f32[504,768]{0,1:T(8,128)S(1)} fusion(f32[504,1149]{1,0:T(8,128)S(1)} %copy-done, f32[1149,768]{0,1:T(8,128)} %all-gather.2.cloned.1.call-done), kind=kOutput, calls=%fused_computation.13 | convolution fusion | flops 5336948736 | bytes 7394400 | tf_op jit(solution)/shard_map/dot_general | solution.py:36
  77.3 44.3 %all_to_all.21 = f32[504,4,192]{0,2,1:T(8,128)S(1)} all-to-all(f32[504,4,192]{0,2,1:T(8,128)S(1)} %bitcast.11), channel_id=1, replica_groups=mesh['row'=4,'col'=16,'layer'=4] {'row'}, dimensions={1} | all-to-all | bytes 3096576 | tf_op jit(solution)/shard_map/all_to_all | solution.py:42
  121.6 2.2 %copy.12 = f32[4,504,192]{1,0,2:T(4,128)} copy(f32[4,504,192]{1,2,0:T(8,128)S(1)} %bitcast.9) | data formatting | bytes 3096576 | tf_op jit(solution)/shard_map/all_to_all | solution.py:42
  123.7 2.9 %reshape.43 = f32[16,126,4,48]{1,0,3,2:T(8,128)} reshape(f32[4,504,192]{1,0,2:T(4,128)} %copy.12) | data formatting | bytes 3096576 | tf_op jit(solution)/shard_map/reshape | solution.py:31
  126.6 3.1 %copy.13 = f32[16,4,126,48]{2,3,1,0:T(8,128)} copy(f32[16,4,126,48]{2,0,3,1:T(8,128)} %bitcast.10) | data formatting | bytes 3096576 | tf_op jit(solution)/shard_map/transpose | solution.py:32
  129.7 0.0 copy-start.2
  129.7 0.0 copy-start.3
  129.7 9.9 %all-to-all-start.1 = ((f32[64,126,48]{1,2,0:T(8,128)}), f32[64,126,48]{1,2,0:T(8,128)}, u32[]{:S(2)}, u32[]{:S(2)}) async-start(f32[64,126,48]{1,2,0:T(8,128)} %bitcast.8), calls=%async_computation.1 | async-start | bytes 3145728 | tf_op jit(solution)/shard_map/all_to_all | solution.py:16
  139.6 0.8 dynamic_slice.7
  140.4 0.8 dynamic_slice.6
  141.2 0.0 copy-done.2
  141.2 0.2 select_reduce_fusion
  141.4 0.0 copy-done.3
  141.4 0.1 select_reduce_fusion.2
  141.5 36.2 %all-to-all-done.1 = f32[64,126,48]{1,2,0:T(8,128)} async-done(((f32[64,126,48]{1,2,0:T(8,128)}), f32[64,126,48]{1,2,0:T(8,128)}, u32[]{:S(2)}, u32[]{:S(2)}) %all-to-all-start.1) | async-done | bytes 1548320 | tf_op jit(solution)/shard_map/all_to_all | solution.py:16
  177.7 1.6 reduce_sum.45
  179.2 0.0 copy-start.1
  179.2 0.7 subtract_divide_fusion
  179.9 0.0 copy-done.1
  (3 shorter events, 0.0 us)
Async XLA Ops:
  7.2 61.8 %copy-start = (f32[504,1149]{1,0:T(8,128)S(1)}, f32[504,1149]{1,0:T(8,128)}, u32[]{:S(2)}) copy-start(f32[504,1149]{1,0:T(8,128)} %param.6) | copy-start | bytes 6949156
  7.2 61.8 %all-gather.2.cloned.1.call-start = ((), (), s32[]{:S(2)}) async-start(), calls=%async_computation.2 | async-start | bytes 4423680 | tf_op jit(solution)/shard_map/all_gather | solution.py:38
  129.7 11.5 %copy-start.2 = (f32[384]{0:T(512)S(1)}, f32[384]{0:T(512)}, u32[]{:S(2)}) copy-start(f32[384]{0:T(512)} %param.9) | copy-start | bytes 4612
  129.7 11.7 %copy-start.3 = (f32[64]{0:T(128)S(1)}, f32[64]{0:T(128)}, u32[]{:S(2)}) copy-start(f32[64]{0:T(128)} %param.8) | copy-start | bytes 772
  129.7 48.0 %all-to-all-start.1 = ((f32[64,126,48]{1,2,0:T(8,128)}), f32[64,126,48]{1,2,0:T(8,128)}, u32[]{:S(2)}, u32[]{:S(2)}) async-start(f32[64,126,48]{1,2,0:T(8,128)} %bitcast.8), calls=%async_computation.1 | async-start | bytes 3145728 | tf_op jit(solution)/shard_map/all_to_all | solution.py:16
  179.2 0.7 copy-start.1
Sparse Core Ops, SparseCore 0:
  9.8 59.1 all-gather.1
where the time goes:
time: 189 us; the launch traced here: 187 us
  waiting for transfers between devices  97.9 us (52%)
  blocking collectives  44.3 us (23%)
  between operations  14.1 us (7%)
  starting transfers between devices  9.96 us (5%)
  local copies, waits for them, and re-layouts  9.7 us (5%)
  matrix products  8.31 us (4%)
  other arithmetic  2.55 us (1%)
    all_gather x1, waiting for transfers between devices, shards(): lax.all_gather(integrals, 'row', axis=1, tiled=True)  61.1 us
    all_to_all x1, blocking collectives, shards(): lax.all_to_all(partial_rows, 'row', split_axis=1, concat_axis=0, tiled=True)  44.3 us
    all_to_all x1, waiting for transfers between devices, summed_on_arrival(): parts = lax.all_to_all(in_blocks(array, dim, count), axis, 0, 0, tiled=True)  36.2 us
    all_to_all x1, starting transfers between devices, summed_on_arrival(): parts = lax.all_to_all(in_blocks(array, dim, count), axis, 0, 0, tiled=True)  9.92 us
    dot_general x1, matrix products, shards(): jnp.dot(amplitudes, lax.all_gather(integrals, 'row', axis=1, tiled=True),...  8.31 us
  transfers between devices with their start and end apart: 2, of which 2 were waited for; matrix products, arithmetic and copies ran while one was open for 1% of the time, Pallas kernels for 0%

commit v1 on v0

v1 whole, which is shorter than its diff:
```python
import functools

import jax
import jax.numpy as jnp
from jax import lax
from jax.experimental import pallas as pl
from jax.experimental.pallas import tpu as pltpu
from jax.sharding import PartitionSpec as P

MESH = pl.DeviceIdType.MESH
F32, BF16 = jnp.float32, jnp.bfloat16

OCC, VIR = 64, 384
ROWS = 504
OWN = 126
EF = 1149
KP = 1152
COLS = 192
SLAB = 48
CH = 6
BLK = 128


def split(value):
    high = value.astype(BF16)
    return high, (value - high.astype(F32)).astype(BF16)


def denominators(occ, vir, col, slab_a, slab_b):
    p = lax.broadcasted_iota(jnp.int32, (BLK, OCC), 0) + col * OWN
    i = lax.broadcasted_iota(jnp.int32, (BLK, OCC), 1)
    first = i * (2 * OCC - 1 - i) // 2
    is_i = (p >= first) & (p < first + OCC - 1 - i)
    j = p[:, :1] + jnp.sum(jnp.where(is_i, i + 1 - first, 0), axis=1, keepdims=True)
    row = lambda mask: jnp.sum(jnp.where(mask, occ, 0.0), axis=1, keepdims=True)
    pair_sum = row(is_i) + row(i == j)
    lane = lax.broadcasted_iota(jnp.int32, (1, VIR), 1)
    vir_a = jnp.sum(jnp.where(lane == slab_a, vir, 0.0), axis=1, keepdims=True)
    b = lax.broadcasted_iota(jnp.int32, (SLAB, VIR), 1)
    q = lax.broadcasted_iota(jnp.int32, (SLAB, VIR), 0) + slab_b
    vir_b = jnp.sum(jnp.where(b == q, vir, 0.0), axis=1, keepdims=True)
    vir_sum = jnp.transpose(jnp.broadcast_to(vir_a + vir_b, (SLAB, BLK)))
    return pair_sum - vir_sum


def kernel(
    a_hbm, b_hbm, occ_ref, vir_ref, ladder_ref, step_ref,
    a_own, a_other, b_own, a_high, a_low, chunks, outgoing, incoming, reduced, landed, denom,
    a_sem, b_sem, core_send, core_recv, z_send, z_recv, xy_send, xy_recv, end_send, end_recv,
):
    row, col, x = lax.axis_index("row"), lax.axis_index("col"), lax.axis_index("layer")
    half, core = row // 2, row % 2
    z, y = col // 4, col % 4
    plane = x * 4 + y

    def device(half_to, z_to, y_to, x_to, core_to=core):
        return (half_to * 2 + core_to, z_to * 4 + y_to, x_to)

    load_b = pltpu.make_async_copy(b_hbm, b_own, b_sem)
    load_b.start()
    load_a = pltpu.make_async_copy(a_hbm, a_own, a_sem)
    load_a.start()

    barrier = pltpu.get_barrier_semaphore()

    def greet(to):
        pl.semaphore_signal(barrier, inc=1, device_id=to, device_id_type=MESH)

    greet(device(half, z, y, x, 1 - core))
    for step in range(1, 8):
        to = lax.rem(half * 4 + z + step, 8)
        greet(device(to // 4, to % 4, y, x))
    for step in range(1, 16):
        to = lax.rem(plane + step, 16)
        greet(device(half, z, to % 4, to // 4))

    load_b.wait()
    for block in range(KP // BLK):
        lanes = pl.ds(block * BLK, BLK)
        if block < KP // BLK - 1:
            part = b_own[lanes, :]
        else:
            part = pltpu.roll(b_own[pl.ds(EF - BLK, BLK), :], BLK - (KP - EF), 0)
            k = lax.broadcasted_iota(jnp.int32, part.shape, 0) + block * BLK
            part = jnp.where(k < EF, part, 0.0)
        part = jnp.transpose(part)
        for owner in range(4):
            for c in range(CH):
                at = owner * SLAB + c * 8
                chunks[c, owner, :, lanes] = part[at : at + 8, :]

    pl.semaphore_wait(barrier, 23)

    def z_copy(c):
        return pltpu.make_async_remote_copy(
            chunks.at[c], chunks.at[CH + c], z_send.at[c], z_recv.at[c],
            device_id=device(1 - half, z, y, x), device_id_type=MESH,
        )

    for c in range(CH):
        z_copy(c).start()

    load_a.wait()
    a_copy = pltpu.make_async_remote_copy(
        a_own, a_other, core_send, core_recv,
        device_id=device(half, z, y, x, 1 - core), device_id_type=MESH,
    )
    a_copy.start()

    def prepare(source, which):
        def block_of(block, masked):
            at = block * BLK if masked else pl.multiple_of(block * BLK, BLK)
            for owner in range(4):
                lanes = pl.ds(at, EF - at if masked else BLK)
                if owner < 3:
                    part = source[pl.ds(owner * OWN, BLK), lanes]
                else:
                    part = pltpu.roll(source[pl.ds(ROWS - BLK, BLK), lanes], OWN, 0)
                if masked:
                    part = jnp.pad(part, ((0, 0), (0, KP - EF)))
                high, low = split(jnp.transpose(part))
                lanes = pl.ds(owner * 256 + which * BLK, BLK)
                a_high[pl.ds(at, BLK), lanes] = high
                a_low[pl.ds(at, BLK), lanes] = low

        @pl.loop(0, KP // BLK - 1)
        def _(block):
            block_of(block, False)

        block_of(KP // BLK - 1, True)

    prepare(a_own, 0)
    denom[...] = denominators(occ_ref[...], vir_ref[...], col, half, core * COLS + x * SLAB)
    a_copy.wait_recv()
    prepare(a_other, 1)

    def xy_copy(c, to):
        return pltpu.make_async_remote_copy(
            outgoing.at[c, to], incoming.at[c, plane], xy_send.at[c], xy_recv.at[c],
            device_id=device(half, z, to % 4, to // 4), device_id_type=MESH,
        )

    def end_copy(c, which, half_to):
        z_to = 2 * half + lax.rem(core + which, 2)
        return z_to, pltpu.make_async_remote_copy(
            reduced.at[c, which], landed.at[lax.rem(c, CH), z], end_send, end_recv,
            device_id=device(half_to, z_to, y, x), device_id_type=MESH,
        )

    def multiply(c):
        b_high, b_low = split(chunks[c].reshape(32, KP))
        both = jnp.concatenate([b_high, b_low], axis=0)
        upper = jnp.dot(both, a_high[...], preferred_element_type=F32)
        lower = jnp.dot(b_high, a_low[...], preferred_element_type=F32)
        value = upper[:32] + (upper[32:] + lower)
        for x_to in range(4):
            for y_to in range(4):
                outgoing[c, x_to * 4 + y_to] = value[8 * x_to : 8 * x_to + 8, 256 * y_to : 256 * y_to + 256]
        incoming[c, plane] = outgoing[c, plane]

        @pl.loop(1, 16)
        def _(step):
            xy_copy(c, lax.rem(plane + step, 16)).start()

    def reduce(c, cross):
        xy_all = pltpu.make_async_remote_copy(
            outgoing.at[c, pl.ds(0, 15)], incoming.at[c, pl.ds(0, 15)], xy_send.at[c], xy_recv.at[c],
            device_id=device(1 - half, z, y, x), device_id_type=MESH,
        )
        xy_all.wait_recv()
        total = jnp.sum(incoming[c], axis=0)
        for which in range(2):
            reduced[c, which] = total[:, which * BLK : which * BLK + BLK]
        for which in range(2):
            z_to, copy = end_copy(c, which, 1 - half if cross else half)
            if cross:
                copy.start()
            else:

                @pl.when(z_to == z)
                def _():
                    landed[lax.rem(c, CH), z] = reduced[c, which]

                @pl.when(z_to != z)
                def _():
                    copy.start()

    @pl.loop(0, 2 * CH)
    def _(c):
        @pl.when(c >= CH)
        def _():
            z_copy(c - CH).wait_recv()

        multiply(c)

        @pl.when(c >= CH)
        def _():
            reduce(c - CH, False)

        @pl.when(c > CH)
        def _():
            reduce(c - 1, True)

    reduce(2 * CH - 1, True)

    def end_all(count):
        return pltpu.make_async_remote_copy(
            landed.at[:, pl.ds(0, count)], landed.at[:, pl.ds(0, count)], end_send, end_recv,
            device_id=device(1 - half, z, y, x), device_id_type=MESH,
        )

    home = z // 2 == half

    @pl.when(home)
    def _():
        end_all(3).wait_recv()

    @pl.when(jnp.logical_not(home))
    def _():
        end_all(4).wait_recv()

    total = jnp.sum(landed[...], axis=1).reshape(SLAB, BLK)
    ladder = jnp.transpose(total)[:OWN, :]
    ladder_ref[...] = ladder
    step_ref[...] = ladder / denom[:OWN, :]

    a_copy.wait_send()
    for c in range(CH):
        z_copy(c).wait_send()

    @pl.loop(0, 2 * CH)
    def _(c):
        pltpu.make_async_remote_copy(
            outgoing.at[c, pl.ds(0, 15)], incoming.at[c, pl.ds(0, 15)], xy_send.at[c], xy_recv.at[c],
            device_id=device(1 - half, z, y, x), device_id_type=MESH,
        ).wait_send()

    end_all(3).wait_send()

    @pl.when(jnp.logical_not(home))
    def _():
        landed_one = landed.at[:, pl.ds(0, 1)]
        pltpu.make_async_remote_copy(
            landed_one, landed_one, end_send, end_recv,
            device_id=device(1 - half, z, y, x), device_id_type=MESH,
        ).wait_send()


def shards(amplitudes, integrals, occ_energy, vir_energy):
    block = jax.ShapeDtypeStruct((OWN, SLAB), F32)
    dma = pltpu.SemaphoreType.DMA
    vmem = pl.BlockSpec(memory_space=pltpu.VMEM)
    hbm = pl.BlockSpec(memory_space=pl.ANY)
    return pl.pallas_call(
        kernel,
        out_shape=(block, block),
        in_specs=[hbm, hbm, vmem, vmem],
        out_specs=(vmem, vmem),
        scratch_shapes=[
            pltpu.VMEM((ROWS, EF), F32),
            pltpu.VMEM((ROWS, EF), F32),
            pltpu.VMEM((EF, COLS), F32),
            pltpu.VMEM((KP, 1024), BF16),
            pltpu.VMEM((KP, 1024), BF16),
            pltpu.VMEM((2 * CH, 4, 8, KP), F32),
            pltpu.VMEM((2 * CH, 16, 8, 256), F32),
            pltpu.VMEM((2 * CH, 16, 8, 256), F32),
            pltpu.VMEM((2 * CH, 2, 8, BLK), F32),
            pltpu.VMEM((CH, 4, 8, BLK), F32),
            pltpu.VMEM((BLK, SLAB), F32),
            dma, dma, dma, dma,
            dma((CH,)), dma((CH,)),
            dma((2 * CH,)), dma((2 * CH,)),
            dma, dma,
        ],
        compiler_params=pltpu.CompilerParams(collective_id=0, has_side_effects=True, vmem_limit_bytes=56 * 2**20),
    )(amplitudes, integrals, occ_energy.reshape(1, OCC), vir_energy.reshape(1, VIR))


def solution(mesh):
    in_specs = (P("row", ("layer", "col")), P(("layer", "col"), "row"), P(), P())
    out_specs = (P("col", ("row", "layer")), P("col", ("row", "layer")))
    return jax.shard_map(shards, mesh=mesh, in_specs=in_specs, out_specs=out_specs, check_vma=False)
```

time: 189 us -> 70.4 us (0.37); the launches traced: 187 us -> 70.1 us
  waiting for transfers between devices: 97.9 us -> 0 us
  Pallas kernels: 0 us -> 62.6 us
  blocking collectives: 44.3 us -> 0 us
  between operations: 14.1 us -> 0.64 us
  starting transfers between devices: 9.96 us -> 0 us
  matrix products: 8.31 us -> 0 us
  local copies, waits for them, and re-layouts: 9.7 us -> 6.85 us
  other arithmetic: 2.55 us -> 0 us
    pallas_call x0 -> x1, Pallas kernels: none -> 62.6 us  [shards(): pl.pallas_call(kernel, out_shape=(block, block), in_specs=[hbm, hbm, vmem...]
    all_gather x1 -> x0, waiting for transfers between devices: 61.1 us -> none  [shards(): lax.all_gather(integrals, 'row', axis=1, tiled=True)]
    all_to_all x1 -> x0, blocking collectives: 44.3 us -> none  [shards(): lax.all_to_all(partial_rows, 'row', split_axis=1, concat_axis=0, tiled=True)]
    all_to_all x1 -> x0, waiting for transfers between devices: 36.2 us -> none  [summed_on_arrival(): parts = lax.all_to_all(in_blocks(array, dim, count), axis, 0, 0, tiled=True)]
    all_to_all x1 -> x0, starting transfers between devices: 9.92 us -> none  [summed_on_arrival(): parts = lax.all_to_all(in_blocks(array, dim, count), axis, 0, 0, tiled=True)]
    dot_general x1 -> x0, matrix products: 8.31 us -> none  [shards(): jnp.dot(amplitudes, lax.all_gather(integrals, 'row', axis=1, tiled=True),...]
    transpose x1 -> x0, local copies, waits for them, and re-layouts: 3.06 us -> none  [owner_blocks(): blocks.transpose(0, 2, 1, 3)]
    pallas_call x0 -> x2, local copies, waits for them, and re-layouts: none -> 3.05 us  [shards(): pl.pallas_call(kernel, out_shape=(block, block), in_specs=[hbm, hbm, vmem...]
  transfers between devices with their start and end apart: 2 -> 0, of which waited for: 2 -> 0; matrix products, arithmetic and copies ran while one was open for 1% -> 0% of each run, Pallas kernels for 0% -> 0%
where the time goes in v1:
time: 70.4 us; the launch traced here: 70.1 us
  Pallas kernels  62.6 us (89%)
  local copies, waits for them, and re-layouts  6.85 us (10%)
    pallas_call x1, Pallas kernels, shards(): pl.pallas_call(kernel, out_shape=(block, block), in_specs=[hbm, hbm, vmem...  62.6 us
    pallas_call x2, local copies, waits for them, and re-layouts, shards(): pl.pallas_call(kernel, out_shape=(block, block), in_specs=[hbm, hbm, vmem...  3.05 us
    unnamed x1, local copies, waits for them, and re-layouts  2.55 us

profile of v1, /device:TPU:64, one launch (start us, length us, event | category | flops | bytes accessed | tf_op | source)
XLA Modules:
  0.0 70.1 jit_solution(15516414303409243381)
XLA Ops:
  0.6 1.2 %reshape.11.vir_ref = f32[1,384]{1,0:T(1,128)} reshape(f32[384]{0:T(512)} %param.7) | data formatting | bytes 3072 | tf_op jit(solution)/shard_map/reshape | solution.py:277
  1.9 2.5 %copy.6.b_hbm = f32[1149,192]{1,0:T(8,128)} copy(f32[1149,192]{0,1:T(8,128)} %param.5) | data formatting | bytes 1764864 | tf_op args[1]
  4.4 62.6 %shard_map.59 = (f32[126,48]{1,0:T(8,128)}, f32[126,48]{1,0:T(8,128)}) custom-call(f32[504,1149]{1,0:T(8,128)} %a_hbm.1, f32[1149,192]{1,0:T(8,128)} %copy.6.b_hbm, f32[1,64]{1,0:T(1,128)} %bitcast.1, f32[1,384]{1,0:T(1,128)} %reshape.11.vir_ref), custom_call_target="tpu_custom_call" | custom-call | tf_op jit(solution)/shard_map/pallas_call | solution.py:254
  67.0 1.5 %copy.7 = f32[126,48]{0,1:T(8,128)} copy(f32[126,48]{1,0:T(8,128)} %get-tuple-element.2) | data formatting | bytes 48384 | tf_op jit(solution)/shard_map/pallas_call | solution.py:254
  68.6 1.5 %copy.8 = f32[126,48]{0,1:T(8,128)} copy(f32[126,48]{1,0:T(8,128)} %get-tuple-element.3) | data formatting | bytes 48384 | tf_op jit(solution)/shard_map/pallas_call | solution.py:254

commit v2 on v1

--- a/solution.py
+++ b/solution.py
@@ -39,13 +39,12 @@
     b = lax.broadcasted_iota(jnp.int32, (SLAB, VIR), 1)
     q = lax.broadcasted_iota(jnp.int32, (SLAB, VIR), 0) + slab_b
     vir_b = jnp.sum(jnp.where(b == q, vir, 0.0), axis=1, keepdims=True)
-    vir_sum = jnp.transpose(jnp.broadcast_to(vir_a + vir_b, (SLAB, BLK)))
-    return pair_sum - vir_sum
+    return jnp.transpose(jnp.broadcast_to(pair_sum, (BLK, BLK)))[:SLAB] - (vir_a + vir_b)
 
 
 def kernel(
-    a_hbm, b_hbm, occ_ref, vir_ref, ladder_ref, step_ref,
-    a_own, a_other, b_own, a_high, a_low, chunks, outgoing, incoming, reduced, landed, denom,
+    a_hbm, b_hbm, occ_ref, vir_ref, ladder_ref, denom_ref,
+    a_own, a_other, a_high, a_low, chunks, outgoing, incoming, reduced, landed,
     a_sem, b_sem, core_send, core_recv, z_send, z_recv, xy_send, xy_recv, end_send, end_recv,
 ):
     row, col, x = lax.axis_index("row"), lax.axis_index("col"), lax.axis_index("layer")
@@ -56,8 +55,11 @@
     def device(half_to, z_to, y_to, x_to, core_to=core):
         return (half_to * 2 + core_to, z_to * 4 + y_to, x_to)
 
-    load_b = pltpu.make_async_copy(b_hbm, b_own, b_sem)
-    load_b.start()
+    loads = [
+        pltpu.make_async_copy(b_hbm.at[:, pl.ds(8 * c, 8), :], chunks.at[c], b_sem.at[c]) for c in range(CH)
+    ]
+    for load in loads:
+        load.start()
     load_a = pltpu.make_async_copy(a_hbm, a_own, a_sem)
     load_a.start()
 
@@ -74,21 +76,6 @@
         to = lax.rem(plane + step, 16)
         greet(device(half, z, to % 4, to // 4))
 
-    load_b.wait()
-    for block in range(KP // BLK):
-        lanes = pl.ds(block * BLK, BLK)
-        if block < KP // BLK - 1:
-            part = b_own[lanes, :]
-        else:
-            part = pltpu.roll(b_own[pl.ds(EF - BLK, BLK), :], BLK - (KP - EF), 0)
-            k = lax.broadcasted_iota(jnp.int32, part.shape, 0) + block * BLK
-            part = jnp.where(k < EF, part, 0.0)
-        part = jnp.transpose(part)
-        for owner in range(4):
-            for c in range(CH):
-                at = owner * SLAB + c * 8
-                chunks[c, owner, :, lanes] = part[at : at + 8, :]
-
     pl.semaphore_wait(barrier, 23)
 
     def z_copy(c):
@@ -98,6 +85,7 @@
         )
 
     for c in range(CH):
+        loads[c].wait()
         z_copy(c).start()
 
     load_a.wait()
@@ -130,7 +118,7 @@
         block_of(KP // BLK - 1, True)
 
     prepare(a_own, 0)
-    denom[...] = denominators(occ_ref[...], vir_ref[...], col, half, core * COLS + x * SLAB)
+    denom_ref[...] = denominators(occ_ref[...].reshape(1, OCC), vir_ref[...].reshape(1, VIR), col, half, core * COLS + x * SLAB)
     a_copy.wait_recv()
     prepare(a_other, 1)
 
@@ -148,7 +136,7 @@
         )
 
     def multiply(c):
-        b_high, b_low = split(chunks[c].reshape(32, KP))
+        b_high, b_low = split(jnp.pad(chunks[c].reshape(32, EF), ((0, 0), (0, KP - EF))))
         both = jnp.concatenate([b_high, b_low], axis=0)
         upper = jnp.dot(both, a_high[...], preferred_element_type=F32)
         lower = jnp.dot(b_high, a_low[...], preferred_element_type=F32)
@@ -219,10 +207,7 @@
     def _():
         end_all(4).wait_recv()
 
-    total = jnp.sum(landed[...], axis=1).reshape(SLAB, BLK)
-    ladder = jnp.transpose(total)[:OWN, :]
-    ladder_ref[...] = ladder
-    step_ref[...] = ladder / denom[:OWN, :]
+    ladder_ref[...] = jnp.sum(landed[...], axis=1).reshape(SLAB, BLK)
 
     a_copy.wait_send()
     for c in range(CH):
@@ -247,11 +232,11 @@
 
 
 def shards(amplitudes, integrals, occ_energy, vir_energy):
-    block = jax.ShapeDtypeStruct((OWN, SLAB), F32)
+    block = jax.ShapeDtypeStruct((SLAB, BLK), F32)
     dma = pltpu.SemaphoreType.DMA
     vmem = pl.BlockSpec(memory_space=pltpu.VMEM)
     hbm = pl.BlockSpec(memory_space=pl.ANY)
-    return pl.pallas_call(
+    ladder, denominator = pl.pallas_call(
         kernel,
         out_shape=(block, block),
         in_specs=[hbm, hbm, vmem, vmem],
@@ -259,22 +244,22 @@
         scratch_shapes=[
             pltpu.VMEM((ROWS, EF), F32),
             pltpu.VMEM((ROWS, EF), F32),
-            pltpu.VMEM((EF, COLS), F32),
             pltpu.VMEM((KP, 1024), BF16),
             pltpu.VMEM((KP, 1024), BF16),
-            pltpu.VMEM((2 * CH, 4, 8, KP), F32),
+            pltpu.VMEM((2 * CH, 4, 8, EF), F32),
             pltpu.VMEM((2 * CH, 16, 8, 256), F32),
             pltpu.VMEM((2 * CH, 16, 8, 256), F32),
             pltpu.VMEM((2 * CH, 2, 8, BLK), F32),
             pltpu.VMEM((CH, 4, 8, BLK), F32),
-            pltpu.VMEM((BLK, SLAB), F32),
-            dma, dma, dma, dma,
+                        dma, dma((CH,)), dma, dma,
             dma((CH,)), dma((CH,)),
             dma((2 * CH,)), dma((2 * CH,)),
             dma, dma,
         ],
         compiler_params=pltpu.CompilerParams(collective_id=0, has_side_effects=True, vmem_limit_bytes=56 * 2**20),
-    )(amplitudes, integrals, occ_energy.reshape(1, OCC), vir_energy.reshape(1, VIR))
+    )(amplitudes, integrals.T.reshape(4, SLAB, EF), occ_energy, vir_energy)
+    ladder = ladder[:, :OWN].T
+    return ladder, ladder / denominator[:, :OWN].T
 
 
 def solution(mesh):

time: 70.4 us -> 64.9 us (0.922)
  local copies, waits for them, and re-layouts: 6.85 us -> 0 us
  other arithmetic: 0 us -> 1.38 us
    pallas_call x2 -> x0, local copies, waits for them, and re-layouts: 3.05 us -> none  [shards(): pl.pallas_call(kernel, out_shape=(block, block), in_specs=[hbm, hbm, vmem...]
    unnamed x1 -> x0, local copies, waits for them, and re-layouts: 2.55 us -> none
    div x0 -> x1, other arithmetic: none -> 1.38 us  [shards(): return (ladder, ladder / denominator[:, :OWN].T)]
    reshape x1 -> x0, local copies, waits for them, and re-layouts: 1.25 us -> none  [shards(): vir_energy.reshape(1, VIR)]
where the time goes in v2:
time: 64.9 us; the launch traced here: 64.7 us
  Pallas kernels  62.7 us (97%)
  other arithmetic  1.38 us (2%)
    pallas_call x1, Pallas kernels, shards(): pl.pallas_call(kernel, out_shape=(block, block), in_specs=[hbm, hbm, vmem...  62.7 us
    div x1, other arithmetic, shards(): return (ladder, ladder / denominator[:, :OWN].T)  1.38 us

profile of v2, /device:TPU:64, one launch (start us, length us, event | category | flops | bytes accessed | tf_op | source)
XLA Modules:
  0.0 64.7 jit_solution(11041819519086581934)
XLA Ops:
  0.6 62.7 %shard_map.59 = (f32[48,128]{1,0:T(8,128)}, f32[48,128]{1,0:T(8,128)}) custom-call(f32[504,1149]{1,0:T(8,128)} %a_hbm.1, f32[4,48,1149]{2,1,0:T(8,128)} %bitcast.8, f32[64]{0:T(128)} %occ_ref.1, f32[384]{0:T(512)} %vir_ref.1), custom_call_target="tpu_custom_call" | custom-call | tf_op jit(solution)/shard_map/pallas_call | solution.py:239
  63.3 1.4 %bitcast_divide_fusion = (f32[126,48]{0,1:T(8,128)}, f32[126,48]{0,1:T(8,128)}) fusion(f32[48,128]{1,0:T(8,128)} %get-tuple-element.5, f32[48,128]{1,0:T(8,128)} %get-tuple-element.4), kind=kLoop, calls=%fused_computation | loop fusion | flops 6048 | bytes 96768 | tf_op jit(solution)/shard_map/div | solution.py:262

commit v3 on v2

v3 whole, which is shorter than its diff:
```python
import jax
import jax.numpy as jnp
from jax import lax
from jax.experimental import pallas as pl
from jax.experimental.pallas import tpu as pltpu
from jax.sharding import PartitionSpec as P

MESH = pl.DeviceIdType.MESH
F32, BF16 = jnp.float32, jnp.bfloat16

OCC, VIR = 64, 384
ROWS = 504
OWN = 126
EF = 1149
KP = 1152
COLS = 192
SLAB = 48
BLK = 128
TILE = 8
WIDE = 2 * BLK
HALVES = ((0, 3), (3, 3))
LAST = ((0, 3), (3, 2), (5, 1))
PIECES = 9
HELD = 6
LOCAL = PIECES


def far_first(i):
    return jnp.where(i == 0, 2, jnp.where(i == 1, 1, jnp.where(i == 2, 3, 0)))


def split(value):
    high = value.astype(BF16)
    return high, (value - high.astype(F32)).astype(BF16)


def denominators(occ, vir, col, slab_a, slab_b):
    p = lax.broadcasted_iota(jnp.int32, (BLK, OCC), 0) + col * OWN
    i = lax.broadcasted_iota(jnp.int32, (BLK, OCC), 1)
    first = i * (2 * OCC - 1 - i) // 2
    is_i = (p >= first) & (p < first + OCC - 1 - i)
    j = p[:, :1] + jnp.sum(jnp.where(is_i, i + 1 - first, 0), axis=1, keepdims=True)
    row = lambda mask: jnp.sum(jnp.where(mask, occ, 0.0), axis=1, keepdims=True)
    pair_sum = row(is_i) + row(i == j)
    lane = lax.broadcasted_iota(jnp.int32, (1, VIR), 1)
    vir_a = jnp.sum(jnp.where(lane == slab_a, vir, 0.0), axis=1, keepdims=True)
    b = lax.broadcasted_iota(jnp.int32, (SLAB, VIR), 1)
    q = lax.broadcasted_iota(jnp.int32, (SLAB, VIR), 0) + slab_b
    vir_b = jnp.sum(jnp.where(b == q, vir, 0.0), axis=1, keepdims=True)
    return jnp.transpose(jnp.broadcast_to(pair_sum, (BLK, BLK)))[:SLAB] - (vir_a + vir_b)


def kernel(
    a_hbm, b_hbm, occ_ref, vir_ref, ladder_ref, denom_ref,
    a_own, a_other, a_high, a_low, b_own, b_far, outgoing, incoming, partial, reduced, landed,
    a_sem, b_sem, core_send, core_recv, z_send, z_recv, xy_send, xy_recv, end_send, end_recv,
):
    row, col, x = lax.axis_index("row"), lax.axis_index("col"), lax.axis_index("layer")
    half, core = row // 2, row % 2
    z, y = col // 4, col % 4
    plane = x * 4 + y
    far = 1 - half

    def device(half_to, z_to, y_to, x_to, core_to=core):
        return (half_to * 2 + core_to, z_to * 4 + y_to, x_to)

    def remote(src, dst, send, recv, to):
        return pltpu.make_async_remote_copy(src, dst, send, recv, device_id=to, device_id_type=MESH)

    load_b = pltpu.make_async_copy(b_hbm, b_own, b_sem)
    load_b.start()
    load_a = pltpu.make_async_copy(a_hbm, a_own, a_sem)
    load_a.start()

    barrier = pltpu.get_barrier_semaphore()

    def greet(to):
        pl.semaphore_signal(barrier, inc=1, device_id=to, device_id_type=MESH)

    greet(device(half, z, y, x, 1 - core))
    for step in range(1, 8):
        to = lax.rem(half * 4 + z + step, 8)
        greet(device(to // 4, to % 4, y, x))
    for step in range(1, 16):
        to = lax.rem(plane + step, 16)
        greet(device(half, z, to % 4, to // 4))

    load_b.wait()
    pl.semaphore_wait(barrier, 23)

    def z_copy(m, distance, first, tiles):
        at = (lax.rem(x + distance, 4), pl.ds(first * TILE, tiles * TILE))
        return remote(b_own.at[at], b_far.at[at], z_send.at[m], z_recv.at[m], device(far, z, y, x))

    z_copies = [
        z_copy(2 * i + j, (2, 1, 3, 0)[i], *piece)
        for i in range(4)
        for j, piece in enumerate(HALVES if i < 3 else LAST)
    ]
    for copy in z_copies[:HELD]:
        copy.start()

    @pl.when(core == 0)
    def _():
        for copy in z_copies[HELD:]:
            copy.start()

    load_a.wait()
    a_copy = remote(a_own, a_other, core_send, core_recv, device(half, z, y, x, 1 - core))
    a_copy.start()

    def prepare(source, which):
        def block_of(block, masked):
            at = block * BLK if masked else pl.multiple_of(block * BLK, BLK)
            for owner in range(4):
                lanes = pl.ds(at, EF - at if masked else BLK)
                if owner < 3:
                    part = source[pl.ds(owner * OWN, BLK), lanes]
                else:
                    part = pltpu.roll(source[pl.ds(ROWS - BLK, BLK), lanes], OWN, 0)
                if masked:
                    part = jnp.pad(part, ((0, 0), (0, KP - EF)))
                high, low = split(jnp.transpose(part))
                lanes = pl.ds(owner * WIDE + which * BLK, BLK)
                a_high[pl.ds(at, BLK), lanes] = high
                a_low[pl.ds(at, BLK), lanes] = low

        @pl.loop(0, KP // BLK - 1)
        def _(block):
            block_of(block, False)

        block_of(KP // BLK - 1, True)

    prepare(a_own, 0)
    denom_ref[...] = denominators(occ_ref[...].reshape(1, OCC), vir_ref[...].reshape(1, VIR), col, half, core * COLS + x * SLAB)
    a_copy.wait_recv()
    prepare(a_other, 1)

    def multiply(source, kind, m, distance, first, tiles):
        x_to = lax.rem(x + distance, 4)
        at = first * TILE
        if not isinstance(at, int):
            at = pl.multiple_of(at, TILE)
        cols = pl.ds(at, tiles * TILE)
        b = jnp.pad(source[x_to, cols, :], ((0, 0), (0, KP - EF)))
        b_high = b.astype(BF16).astype(F32)
        both = jnp.concatenate([b_high, b - b_high], axis=0).astype(BF16)
        for step in (2, 1, 3, 0):
            y_to = lax.rem(y + step, 4)
            lanes = pl.ds(pl.multiple_of(y_to * WIDE, WIDE), WIDE)
            upper = jnp.dot(both, a_high[:, lanes], preferred_element_type=F32)
            lower = jnp.dot(both, a_low[:, lanes], preferred_element_type=F32)
            n = tiles * TILE
            outgoing[kind, x_to, y_to, cols, :] = upper[:n] + (upper[n:] + (lower[:n] + lower[n:]))

            def send():
                remote(
                    outgoing.at[kind, x_to, y_to, cols], incoming.at[kind, plane, cols],
                    xy_send.at[m], xy_recv.at[m], device(half, z, y_to, x_to),
                ).start()

            if step:
                send()
            elif isinstance(distance, int):
                incoming[kind, plane, cols, :] = outgoing[kind, x_to, y_to, cols, :]
            else:

                @pl.when(distance == 0)
                def _():
                    incoming[kind, plane, cols, :] = outgoing[kind, x_to, y_to, cols, :]

                @pl.when(distance != 0)
                def _():
                    send()

    def xy_all(kind, m, tiles, count):
        blocks = (kind, pl.ds(0, count), pl.ds(0, tiles * TILE))
        return remote(incoming.at[blocks], incoming.at[blocks], xy_send.at[m], xy_recv.at[m], device(far, z, y, x))

    def end_copy(kind, which, cols):
        z_to = 2 * half + lax.rem(core + which, 2)
        half_to = far if kind else half
        return z_to, lambda: remote(
            reduced.at[kind, which, cols], landed.at[z, cols], end_send, end_recv, device(half_to, z_to, y, x)
        ).start()

    @pl.loop(0, 4)
    def _(i):
        multiply(b_own, 0, LOCAL + i, far_first(i), 0, 6)

    def finish_local():
        for i in range(4):
            xy_all(0, LOCAL + i, 6, 4 if i < 3 else 3).wait_recv()
        total = jnp.sum(incoming[0], axis=0)
        for which in range(2):
            reduced[0, which] = total[:, which * BLK : which * BLK + BLK]
        for which in range(2):
            z_to, send = end_copy(0, which, pl.ds(0, SLAB))

            @pl.when(z_to == z)
            def _():
                landed[z] = reduced[0, which]

            @pl.when(z_to != z)
            def _():
                send()

    @pl.loop(0, 7)
    def _(m):
        i = m // 2
        z_copy(m, far_first(i), 0, 3).wait_recv()
        @pl.when((core == 1) & (m == HELD - 1))
        def _():
            for copy in z_copies[HELD:]:
                copy.start()

        multiply(b_far, 1, m, far_first(i), 3 * lax.rem(m, 2), 3)

        @pl.when(m == 2)
        def _():
            finish_local()

    def slot(step):
        return lax.rem(x + step, 4) * 4

    for m in range(6):
        xy_all(1, m, 3, 4).wait_recv()
    total = jnp.sum(incoming[1, pl.ds(slot(1), 4)], axis=0)
    for step in (2, 3):
        total += jnp.sum(incoming[1, pl.ds(slot(step), 4)], axis=0)
    partial[...] = total

    def finish(j):
        first, tiles = LAST[j]
        cols = pl.ds(first * TILE, tiles * TILE)
        xy_all(1, 6 + j, tiles, 3).wait_recv()
        total = partial[cols, :] + jnp.sum(incoming[1, pl.ds(slot(0), 4), cols], axis=0)
        for which in range(2):
            reduced[1, which, cols, :] = total[:, which * BLK : which * BLK + BLK]
            end_copy(1, which, cols)[1]()

    for j in (1, 2):
        z_copies[6 + j].wait_recv()
        multiply(b_far, 1, 6 + j, 0, *LAST[j])
        if j == 1:
            finish(0)
    finish(1)
    finish(2)

    def end_all(count):
        blocks = landed.at[pl.ds(0, count)]
        return remote(blocks, blocks, end_send, end_recv, device(far, z, y, x))

    home = z // 2 == half

    @pl.when(home)
    def _():
        end_all(3).wait_recv()

    @pl.when(jnp.logical_not(home))
    def _():
        end_all(4).wait_recv()

    ladder_ref[...] = jnp.sum(landed[...], axis=0)

    a_copy.wait_send()
    for copy in z_copies:
        copy.wait_send()
    for m in range(PIECES):
        xy_all(1, m, 3 if m < 6 else LAST[m - 6][1], 4 if m < 6 else 3).wait_send()
    for i in range(4):
        xy_all(0, LOCAL + i, 6, 4 if i < 3 else 3).wait_send()
    end_all(3).wait_send()

    @pl.when(jnp.logical_not(home))
    def _():
        end_all(1).wait_send()


def shards(amplitudes, integrals, occ_energy, vir_energy):
    block = jax.ShapeDtypeStruct((SLAB, BLK), F32)
    dma = pltpu.SemaphoreType.DMA
    vmem = pl.BlockSpec(memory_space=pltpu.VMEM)
    hbm = pl.BlockSpec(memory_space=pl.ANY)
    ladder, denominator = pl.pallas_call(
        kernel,
        out_shape=(block, block),
        in_specs=[hbm, hbm, vmem, vmem],
        out_specs=(vmem, vmem),
        scratch_shapes=[
            pltpu.VMEM((ROWS, EF), F32),
            pltpu.VMEM((ROWS, EF), F32),
            pltpu.VMEM((KP, 4 * WIDE), BF16),
            pltpu.VMEM((KP, 4 * WIDE), BF16),
            pltpu.VMEM((4, SLAB, EF), F32),
            pltpu.VMEM((4, SLAB, EF), F32),
            pltpu.VMEM((2, 4, 4, SLAB, WIDE), F32),
            pltpu.VMEM((2, 16, SLAB, WIDE), F32),
            pltpu.VMEM((SLAB, WIDE), F32),
            pltpu.VMEM((2, 2, SLAB, BLK), F32),
            pltpu.VMEM((4, SLAB, BLK), F32),
            dma, dma, dma, dma,
            dma((PIECES,)), dma((PIECES,)),
            dma((PIECES + 4,)), dma((PIECES + 4,)),
            dma, dma,
        ],
        compiler_params=pltpu.CompilerParams(collective_id=0, has_side_effects=True, vmem_limit_bytes=56 * 2**20),
    )(amplitudes, integrals.T.reshape(4, SLAB, EF), occ_energy, vir_energy)
    ladder = ladder[:, :OWN].T
    return ladder, ladder / denominator[:, :OWN].T


def solution(mesh):
    in_specs = (P("row", ("layer", "col")), P(("layer", "col"), "row"), P(), P())
    out_specs = (P("col", ("row", "layer")), P("col", ("row", "layer")))
    return jax.shard_map(shards, mesh=mesh, in_specs=in_specs, out_specs=out_specs, check_vma=False)
```

time: 64.9 us -> 62.3 us (0.960)
  Pallas kernels: 62.7 us -> 59.6 us
    pallas_call x1, Pallas kernels: 62.7 us -> 59.6 us  [shards(): pl.pallas_call(kernel, out_shape=(block, block), in_specs=[hbm, hbm, vmem...]
where the time goes in v3:
time: 62.3 us; the launch traced here: 61.6 us
  Pallas kernels  59.6 us (96%)
  other arithmetic  1.38 us (2%)
  between operations  0.64 us (1%)
    pallas_call x1, Pallas kernels, shards(): pl.pallas_call(kernel, out_shape=(block, block), in_specs=[hbm, hbm, vmem...  59.6 us
    div x1, other arithmetic, shards(): return (ladder, ladder / denominator[:, :OWN].T)  1.38 us

profile of v3, /device:TPU:64, one launch (start us, length us, event | category | flops | bytes accessed | tf_op | source)
XLA Modules:
  0.0 61.6 jit_solution(6915393317976065541)
XLA Ops:
  0.6 59.6 %shard_map.59 = (f32[48,128]{1,0:T(8,128)}, f32[48,128]{1,0:T(8,128)}) custom-call(f32[504,1149]{1,0:T(8,128)} %a_hbm.1, f32[4,48,1149]{2,1,0:T(8,128)} %bitcast.8, f32[64]{0:T(128)} %occ_ref.1, f32[384]{0:T(512)} %vir_ref.1), custom_call_target="tpu_custom_call" | custom-call | tf_op jit(solution)/shard_map/pallas_call | solution.py:285
  60.2 1.4 %bitcast_divide_fusion = (f32[126,48]{0,1:T(8,128)}, f32[126,48]{0,1:T(8,128)}) fusion(f32[48,128]{1,0:T(8,128)} %get-tuple-element.5, f32[48,128]{1,0:T(8,128)} %get-tuple-element.4), kind=kLoop, calls=%fused_computation | loop fusion | flops 6048 | bytes 96768 | tf_op jit(solution)/shard_map/div | solution.py:310

commit v4 on v3

--- a/solution.py
+++ b/solution.py
@@ -51,9 +51,9 @@
 
 
 def kernel(
-    a_hbm, b_hbm, occ_ref, vir_ref, ladder_ref, denom_ref,
-    a_own, a_other, a_high, a_low, b_own, b_far, outgoing, incoming, partial, reduced, landed,
-    a_sem, b_sem, core_send, core_recv, z_send, z_recv, xy_send, xy_recv, end_send, end_recv,
+    a_hbm, b_hbm, occ_hbm, vir_hbm, ladder_ref, denom_ref,
+    a_own, a_other, a_high, a_low, b_own, b_far, outgoing, incoming, partial, reduced, landed, occ_ref, vir_ref,
+    a_sem, b_sem, e_sem, core_send, core_recv, z_send, z_recv, xy_send, xy_recv, end_send, end_recv,
 ):
     row, col, x = lax.axis_index("row"), lax.axis_index("col"), lax.axis_index("layer")
     half, core = row // 2, row % 2
@@ -67,25 +67,32 @@
     def remote(src, dst, send, recv, to):
         return pltpu.make_async_remote_copy(src, dst, send, recv, device_id=to, device_id_type=MESH)
 
-    load_b = pltpu.make_async_copy(b_hbm, b_own, b_sem)
-    load_b.start()
+    loads = []
+    for i, distance in enumerate((2, 1, 3, 0)):
+        owner = lax.rem(x + distance, 4)
+        loads.append(pltpu.make_async_copy(b_hbm.at[owner], b_own.at[owner], b_sem.at[i]))
+        loads[i].start()
     load_a = pltpu.make_async_copy(a_hbm, a_own, a_sem)
     load_a.start()
+    load_e = [
+        pltpu.make_async_copy(occ_hbm, occ_ref, e_sem.at[0]), pltpu.make_async_copy(vir_hbm, vir_ref, e_sem.at[1])
+    ]
+    for load in load_e:
+        load.start()
 
     barrier = pltpu.get_barrier_semaphore()
 
     def greet(to):
         pl.semaphore_signal(barrier, inc=1, device_id=to, device_id_type=MESH)
 
-    greet(device(half, z, y, x, 1 - core))
-    for step in range(1, 8):
+    for step in (4, 3, 5, 2, 6, 1, 7):
         to = lax.rem(half * 4 + z + step, 8)
         greet(device(to // 4, to % 4, y, x))
     for step in range(1, 16):
         to = lax.rem(plane + step, 16)
         greet(device(half, z, to % 4, to // 4))
-
-    load_b.wait()
+    greet(device(half, z, y, x, 1 - core))
+
     pl.semaphore_wait(barrier, 23)
 
     def z_copy(m, distance, first, tiles):
@@ -97,8 +104,11 @@
         for i in range(4)
         for j, piece in enumerate(HALVES if i < 3 else LAST)
     ]
-    for copy in z_copies[:HELD]:
-        copy.start()
+    for m in range(HELD):
+        if m % 2 == 0:
+            loads[m // 2].wait()
+        z_copies[m].start()
+    loads[3].wait()
 
     @pl.when(core == 0)
     def _():
@@ -132,6 +142,8 @@
         block_of(KP // BLK - 1, True)
 
     prepare(a_own, 0)
+    for load in load_e:
+        load.wait()
     denom_ref[...] = denominators(occ_ref[...].reshape(1, OCC), vir_ref[...].reshape(1, VIR), col, half, core * COLS + x * SLAB)
     a_copy.wait_recv()
     prepare(a_other, 1)
@@ -281,11 +293,11 @@
     block = jax.ShapeDtypeStruct((SLAB, BLK), F32)
     dma = pltpu.SemaphoreType.DMA
     vmem = pl.BlockSpec(memory_space=pltpu.VMEM)
-    hbm = pl.BlockSpec(memory_space=pl.ANY)
+    hbm = pl.BlockSpec(memory_space=pltpu.HBM)
     ladder, denominator = pl.pallas_call(
         kernel,
         out_shape=(block, block),
-        in_specs=[hbm, hbm, vmem, vmem],
+        in_specs=[hbm] * 4,
         out_specs=(vmem, vmem),
         scratch_shapes=[
             pltpu.VMEM((ROWS, EF), F32),
@@ -299,13 +311,15 @@
             pltpu.VMEM((SLAB, WIDE), F32),
             pltpu.VMEM((2, 2, SLAB, BLK), F32),
             pltpu.VMEM((4, SLAB, BLK), F32),
-            dma, dma, dma, dma,
+            pltpu.VMEM((OCC,), F32),
+            pltpu.VMEM((VIR,), F32),
+            dma, dma((4,)), dma((2,)), dma, dma,
             dma((PIECES,)), dma((PIECES,)),
             dma((PIECES + 4,)), dma((PIECES + 4,)),
             dma, dma,
         ],
-        compiler_params=pltpu.CompilerParams(collective_id=0, has_side_effects=True, vmem_limit_bytes=56 * 2**20),
-    )(amplitudes, integrals.T.reshape(4, SLAB, EF), occ_energy, vir_energy)
+        compiler_params=pltpu.CompilerParams(collective_id=0, has_side_effects=True, vmem_limit_bytes=20 * 2**20),
+    )(*[pltpu.with_memory_space_constraint(v, pltpu.HBM) for v in (amplitudes, integrals.T.reshape(4, SLAB, EF), occ_energy, vir_energy)])
     ladder = ladder[:, :OWN].T
     return ladder, ladder / denominator[:, :OWN].T
 

time: 62.3 us -> 61 us (0.979)
  Pallas kernels: 59.6 us -> 58.6 us
  other arithmetic: 1.38 us -> 0.62 us
    pallas_call x1, Pallas kernels: 59.6 us -> 58.6 us  [shards(): pl.pallas_call(kernel, out_shape=(block, block), in_specs=[hbm] * 4, out_...]
    div x1, other arithmetic: 1.38 us -> 0.62 us  [shards(): return (ladder, ladder / denominator[:, :OWN].T)]
where the time goes in v4:
time: 61 us; the launch traced here: 59.9 us
  Pallas kernels  58.6 us (96%)
  between operations  0.64 us (1%)
  other arithmetic  0.62 us (1%)
    pallas_call x1, Pallas kernels, shards(): pl.pallas_call(kernel, out_shape=(block, block), in_specs=[hbm] * 4, out_...  58.6 us

profile of v4, /device:TPU:64, one launch (start us, length us, event | category | flops | bytes accessed | tf_op | source)
XLA Modules:
  0.0 59.9 jit_solution(10478956656857577504)
XLA Ops:
  0.6 58.6 %shard_map.59 = (f32[48,128]{1,0:T(8,128)S(1)}, f32[48,128]{1,0:T(8,128)S(1)}) custom-call(f32[504,1149]{1,0:T(8,128)} %a_hbm.1, f32[4,48,1149]{2,1,0:T(8,128)} %bitcast.8, f32[64]{0:T(128)} %occ_hbm.1, f32[384]{0:T(512)} %vir_hbm.1), custom_call_target="tpu_custom_call" | custom-call | tf_op jit(solution)/shard_map/pallas_call | solution.py:297
  59.2 0.6 %bitcast_divide_fusion = (f32[126,48]{0,1:T(8,128)}, f32[126,48]{0,1:T(8,128)}) fusion(f32[48,128]{1,0:T(8,128)S(1)} %get-tuple-element.5, f32[48,128]{1,0:T(8,128)S(1)} %get-tuple-element.4), kind=kLoop, calls=%fused_computation | loop fusion | flops 6048 | bytes 96768 | tf_op jit(solution)/shard_map/div | solution.py:324

commit v5 on v4

--- a/solution.py
+++ b/solution.py
@@ -21,6 +21,7 @@
 HALVES = ((0, 3), (3, 3))
 LAST = ((0, 3), (3, 2), (5, 1))
 PIECES = 9
+TAIL = slice(LAST[2][0] * TILE, SLAB)
 HELD = 6
 LOCAL = PIECES
 
@@ -52,8 +53,8 @@
 
 def kernel(
     a_hbm, b_hbm, occ_hbm, vir_hbm, ladder_ref, denom_ref,
-    a_own, a_other, a_high, a_low, b_own, b_far, outgoing, incoming, partial, reduced, landed, occ_ref, vir_ref,
-    a_sem, b_sem, e_sem, core_send, core_recv, z_send, z_recv, xy_send, xy_recv, end_send, end_recv,
+    a_own, a_other, a_high, a_low, b_own, b_far, outgoing, incoming, partial, reduced, landed, direct_in, occ_ref, vir_ref,
+    a_sem, b_sem, e_sem, core_send, core_recv, z_send, z_recv, xy_send, xy_recv, end_send, end_recv, direct_send, direct_recv,
 ):
     row, col, x = lax.axis_index("row"), lax.axis_index("col"), lax.axis_index("layer")
     half, core = row // 2, row % 2
@@ -92,8 +93,12 @@
         to = lax.rem(plane + step, 16)
         greet(device(half, z, to % 4, to // 4))
     greet(device(half, z, y, x, 1 - core))
-
-    pl.semaphore_wait(barrier, 23)
+    for y_step in range(1, 4):
+        for step in range(1, 8):
+            to = lax.rem(half * 4 + z + step, 8)
+            greet(device(to // 4, to % 4, lax.rem(y + y_step, 4), x))
+
+    pl.semaphore_wait(barrier, 44)
 
     def z_copy(m, distance, first, tiles):
         at = (lax.rem(x + distance, 4), pl.ds(first * TILE, tiles * TILE))
@@ -148,7 +153,10 @@
     a_copy.wait_recv()
     prepare(a_other, 1)
 
-    def multiply(source, kind, m, distance, first, tiles):
+    def z_of(which):
+        return 2 * half + lax.rem(core + which, 2)
+
+    def multiply(source, kind, m, distance, first, tiles, direct=False):
         x_to = lax.rem(x + distance, 4)
         at = first * TILE
         if not isinstance(at, int):
@@ -171,7 +179,13 @@
                     xy_send.at[m], xy_recv.at[m], device(half, z, y_to, x_to),
                 ).start()
 
-            if step:
+            if direct:
+                for which in range(2):
+                    remote(
+                        outgoing.at[kind, x_to, y_to, cols, pl.ds(which * BLK, BLK)], direct_in.at[y * 4 + z],
+                        direct_send, direct_recv, device(far, z_of(which), y_to, x),
+                    ).start()
+            elif step:
                 send()
             elif isinstance(distance, int):
                 incoming[kind, plane, cols, :] = outgoing[kind, x_to, y_to, cols, :]
@@ -190,7 +204,7 @@
         return remote(incoming.at[blocks], incoming.at[blocks], xy_send.at[m], xy_recv.at[m], device(far, z, y, x))
 
     def end_copy(kind, which, cols):
-        z_to = 2 * half + lax.rem(core + which, 2)
+        z_to = z_of(which)
         half_to = far if kind else half
         return z_to, lambda: remote(
             reduced.at[kind, which, cols], landed.at[z, cols], end_send, end_recv, device(half_to, z_to, y, x)
@@ -248,38 +262,50 @@
         xy_all(1, 6 + j, tiles, 3).wait_recv()
         total = partial[cols, :] + jnp.sum(incoming[1, pl.ds(slot(0), 4), cols], axis=0)
         for which in range(2):
-            reduced[1, which, cols, :] = total[:, which * BLK : which * BLK + BLK]
+            lanes = slice(which * BLK, which * BLK + BLK)
+            reduced[1, which, cols, :] = total[:, lanes]
+            if j == 1:
+                reduced[1, which, TAIL, :] = partial[TAIL, lanes]
+        if j == 1:
+            cols = pl.ds(first * TILE, SLAB - first * TILE)
+        for which in range(2):
             end_copy(1, which, cols)[1]()
 
     for j in (1, 2):
         z_copies[6 + j].wait_recv()
-        multiply(b_far, 1, 6 + j, 0, *LAST[j])
+        multiply(b_far, 1, 6 + j, 0, *LAST[j], direct=j == 2)
         if j == 1:
             finish(0)
     finish(1)
-    finish(2)
 
     def end_all(count):
         blocks = landed.at[pl.ds(0, count)]
         return remote(blocks, blocks, end_send, end_recv, device(far, z, y, x))
 
+    def direct_all(count):
+        blocks = direct_in.at[pl.ds(0, count)]
+        return remote(blocks, blocks, direct_send, direct_recv, device(far, z, y, x))
+
     home = z // 2 == half
 
     @pl.when(home)
     def _():
         end_all(3).wait_recv()
+        ladder_ref[...] = jnp.sum(landed[...], axis=0)
 
     @pl.when(jnp.logical_not(home))
     def _():
         end_all(4).wait_recv()
-
-    ladder_ref[...] = jnp.sum(landed[...], axis=0)
+        ladder_ref[...] = jnp.sum(landed[...], axis=0)
+        direct_all(16).wait_recv()
+        ladder_ref[TAIL, :] += jnp.sum(direct_in[...], axis=0)
 
     a_copy.wait_send()
     for copy in z_copies:
         copy.wait_send()
-    for m in range(PIECES):
+    for m in range(PIECES - 1):
         xy_all(1, m, 3 if m < 6 else LAST[m - 6][1], 4 if m < 6 else 3).wait_send()
+    direct_all(8).wait_send()
     for i in range(4):
         xy_all(0, LOCAL + i, 6, 4 if i < 3 else 3).wait_send()
     end_all(3).wait_send()
@@ -311,12 +337,13 @@
             pltpu.VMEM((SLAB, WIDE), F32),
             pltpu.VMEM((2, 2, SLAB, BLK), F32),
             pltpu.VMEM((4, SLAB, BLK), F32),
+            pltpu.VMEM((16, TILE * LAST[2][1], BLK), F32),
             pltpu.VMEM((OCC,), F32),
             pltpu.VMEM((VIR,), F32),
             dma, dma((4,)), dma((2,)), dma, dma,
             dma((PIECES,)), dma((PIECES,)),
             dma((PIECES + 4,)), dma((PIECES + 4,)),
-            dma, dma,
+            dma, dma, dma, dma,
         ],
         compiler_params=pltpu.CompilerParams(collective_id=0, has_side_effects=True, vmem_limit_bytes=20 * 2**20),
     )(*[pltpu.with_memory_space_constraint(v, pltpu.HBM) for v in (amplitudes, integrals.T.reshape(4, SLAB, EF), occ_energy, vir_energy)])

time: 61 us -> 60.6 us (level)
  no operation moved by 1% of the time
where the time goes in v5:
time: 60.6 us; the launch traced here: 60 us
  Pallas kernels  58.7 us (97%)
  between operations  0.64 us (1%)
  other arithmetic  0.62 us (1%)
    pallas_call x1, Pallas kernels, shards(): pl.pallas_call(kernel, out_shape=(block, block), in_specs=[hbm] * 4, out_...  58.7 us

profile of v5, /device:TPU:64, one launch (start us, length us, event | category | flops | bytes accessed | tf_op | source)
XLA Modules:
  0.0 60.0 jit_solution(1095890418483223830)
XLA Ops:
  0.6 58.7 %shard_map.59 = (f32[48,128]{1,0:T(8,128)S(1)}, f32[48,128]{1,0:T(8,128)S(1)}) custom-call(f32[504,1149]{1,0:T(8,128)} %a_hbm.1, f32[4,48,1149]{2,1,0:T(8,128)} %bitcast.8, f32[64]{0:T(128)} %occ_hbm.1, f32[384]{0:T(512)} %vir_hbm.1), custom_call_target="tpu_custom_call" | custom-call | tf_op jit(solution)/shard_map/pallas_call | solution.py:323
  59.3 0.6 %bitcast_divide_fusion = (f32[126,48]{0,1:T(8,128)}, f32[126,48]{0,1:T(8,128)}) fusion(f32[48,128]{1,0:T(8,128)S(1)} %get-tuple-element.5, f32[48,128]{1,0:T(8,128)S(1)} %get-tuple-element.4), kind=kLoop, calls=%fused_computation | loop fusion | flops 6048 | bytes 96768 | tf_op jit(solution)/shard_map/div | solution.py:351

commit v6 on v5

--- a/solution.py
+++ b/solution.py
@@ -68,6 +68,23 @@
     def remote(src, dst, send, recv, to):
         return pltpu.make_async_remote_copy(src, dst, send, recv, device_id=to, device_id_type=MESH)
 
+    barrier = pltpu.get_barrier_semaphore()
+
+    def greet(to):
+        pl.semaphore_signal(barrier, inc=1, device_id=to, device_id_type=MESH)
+
+    for step in (4, 3, 5, 2, 6, 1, 7):
+        to = lax.rem(half * 4 + z + step, 8)
+        greet(device(to // 4, to % 4, y, x))
+    for step in range(1, 16):
+        to = lax.rem(plane + step, 16)
+        greet(device(half, z, to % 4, to // 4))
+    greet(device(half, z, y, x, 1 - core))
+    for y_step in range(1, 4):
+        for step in range(1, 8):
+            to = lax.rem(half * 4 + z + step, 8)
+            greet(device(to // 4, to % 4, lax.rem(y + y_step, 4), x))
+
     loads = []
     for i, distance in enumerate((2, 1, 3, 0)):
         owner = lax.rem(x + distance, 4)
@@ -80,23 +97,6 @@
     ]
     for load in load_e:
         load.start()
-
-    barrier = pltpu.get_barrier_semaphore()
-
-    def greet(to):
-        pl.semaphore_signal(barrier, inc=1, device_id=to, device_id_type=MESH)
-
-    for step in (4, 3, 5, 2, 6, 1, 7):
-        to = lax.rem(half * 4 + z + step, 8)
-        greet(device(to // 4, to % 4, y, x))
-    for step in range(1, 16):
-        to = lax.rem(plane + step, 16)
-        greet(device(half, z, to % 4, to // 4))
-    greet(device(half, z, y, x, 1 - core))
-    for y_step in range(1, 4):
-        for step in range(1, 8):
-            to = lax.rem(half * 4 + z + step, 8)
-            greet(device(to // 4, to % 4, lax.rem(y + y_step, 4), x))
 
     pl.semaphore_wait(barrier, 44)
 

time: 60.6 us -> 60.3 us (level)
  no operation moved by 1% of the time
where the time goes in v6:
time: 60.3 us; the launch traced here: 59.8 us
  Pallas kernels  58.6 us (97%)
  between operations  0.64 us (1%)
  other arithmetic  0.62 us (1%)
    pallas_call x1, Pallas kernels, shards(): pl.pallas_call(kernel, out_shape=(block, block), in_specs=[hbm] * 4, out_...  58.6 us

profile of v6, /device:TPU:64, one launch (start us, length us, event | category | flops | bytes accessed | tf_op | source)
XLA Modules:
  0.0 59.8 jit_solution(8713056348964363561)
XLA Ops:
  0.6 58.6 %shard_map.59 = (f32[48,128]{1,0:T(8,128)S(1)}, f32[48,128]{1,0:T(8,128)S(1)}) custom-call(f32[504,1149]{1,0:T(8,128)} %a_hbm.1, f32[4,48,1149]{2,1,0:T(8,128)} %bitcast.8, f32[64]{0:T(128)} %occ_hbm.1, f32[384]{0:T(512)} %vir_hbm.1), custom_call_target="tpu_custom_call" | custom-call | tf_op jit(solution)/shard_map/pallas_call | solution.py:323
  59.2 0.6 %bitcast_divide_fusion = (f32[126,48]{0,1:T(8,128)}, f32[126,48]{0,1:T(8,128)}) fusion(f32[48,128]{1,0:T(8,128)S(1)} %get-tuple-element.5, f32[48,128]{1,0:T(8,128)S(1)} %get-tuple-element.4), kind=kLoop, calls=%fused_computation | loop fusion | flops 6048 | bytes 96768 | tf_op jit(solution)/shard_map/div | solution.py:351

commit v7 on v5

--- a/solution.py
+++ b/solution.py
@@ -286,6 +286,14 @@
         blocks = direct_in.at[pl.ds(0, count)]
         return remote(blocks, blocks, direct_send, direct_recv, device(far, z, y, x))
 
+    a_copy.wait_send()
+    for copy in z_copies:
+        copy.wait_send()
+    for m in range(PIECES - 1):
+        xy_all(1, m, 3 if m < 6 else LAST[m - 6][1], 4 if m < 6 else 3).wait_send()
+    for i in range(4):
+        xy_all(0, LOCAL + i, 6, 4 if i < 3 else 3).wait_send()
+
     home = z // 2 == half
 
     @pl.when(home)
@@ -300,14 +308,7 @@
         direct_all(16).wait_recv()
         ladder_ref[TAIL, :] += jnp.sum(direct_in[...], axis=0)
 
-    a_copy.wait_send()
-    for copy in z_copies:
-        copy.wait_send()
-    for m in range(PIECES - 1):
-        xy_all(1, m, 3 if m < 6 else LAST[m - 6][1], 4 if m < 6 else 3).wait_send()
     direct_all(8).wait_send()
-    for i in range(4):
-        xy_all(0, LOCAL + i, 6, 4 if i < 3 else 3).wait_send()
     end_all(3).wait_send()
 
     @pl.when(jnp.logical_not(home))

time: 60.6 us -> 60.5 us (level)
  no operation moved by 1% of the time
where the time goes in v7:
time: 60.5 us; the launch traced here: 59.9 us
  Pallas kernels  58.7 us (97%)
  between operations  0.64 us (1%)
  other arithmetic  0.62 us (1%)
    pallas_call x1, Pallas kernels, shards(): pl.pallas_call(kernel, out_shape=(block, block), in_specs=[hbm] * 4, out_...  58.7 us

profile of v7, /device:TPU:64, one launch (start us, length us, event | category | flops | bytes accessed | tf_op | source)
XLA Modules:
  0.0 59.9 jit_solution(7606223666153164620)
XLA Ops:
  0.6 58.7 %shard_map.59 = (f32[48,128]{1,0:T(8,128)S(1)}, f32[48,128]{1,0:T(8,128)S(1)}) custom-call(f32[504,1149]{1,0:T(8,128)} %a_hbm.1, f32[4,48,1149]{2,1,0:T(8,128)} %bitcast.8, f32[64]{0:T(128)} %occ_hbm.1, f32[384]{0:T(512)} %vir_hbm.1), custom_call_target="tpu_custom_call" | custom-call | tf_op jit(solution)/shard_map/pallas_call | solution.py:324
  59.3 0.6 %bitcast_divide_fusion = (f32[126,48]{0,1:T(8,128)}, f32[126,48]{0,1:T(8,128)}) fusion(f32[48,128]{1,0:T(8,128)S(1)} %get-tuple-element.5, f32[48,128]{1,0:T(8,128)S(1)} %get-tuple-element.4), kind=kLoop, calls=%fused_computation | loop fusion | flops 6048 | bytes 96768 | tf_op jit(solution)/shard_map/div | solution.py:352

commit v8 on v5

--- a/solution.py
+++ b/solution.py
@@ -264,12 +264,12 @@
         for which in range(2):
             lanes = slice(which * BLK, which * BLK + BLK)
             reduced[1, which, cols, :] = total[:, lanes]
-            if j == 1:
+            if j == 0:
                 reduced[1, which, TAIL, :] = partial[TAIL, lanes]
-        if j == 1:
-            cols = pl.ds(first * TILE, SLAB - first * TILE)
         for which in range(2):
             end_copy(1, which, cols)[1]()
+            if j == 0:
+                end_copy(1, which, pl.ds(TAIL.start, SLAB - TAIL.start))[1]()
 
     for j in (1, 2):
         z_copies[6 + j].wait_recv()

time: 60.6 us -> 60.7 us (level)
  no operation moved by 1% of the time
where the time goes in v8:
time: 60.7 us; the launch traced here: 59.9 us
  Pallas kernels  58.7 us (97%)
  between operations  0.64 us (1%)
  other arithmetic  0.62 us (1%)
    pallas_call x1, Pallas kernels, shards(): pl.pallas_call(kernel, out_shape=(block, block), in_specs=[hbm] * 4, out_...  58.7 us

profile of v8, /device:TPU:64, one launch (start us, length us, event | category | flops | bytes accessed | tf_op | source)
XLA Modules:
  0.0 59.9 jit_solution(3855526170854355003)
XLA Ops:
  0.6 58.7 %shard_map.59 = (f32[48,128]{1,0:T(8,128)S(1)}, f32[48,128]{1,0:T(8,128)S(1)}) custom-call(f32[504,1149]{1,0:T(8,128)} %a_hbm.1, f32[4,48,1149]{2,1,0:T(8,128)} %bitcast.8, f32[64]{0:T(128)} %occ_hbm.1, f32[384]{0:T(512)} %vir_hbm.1), custom_call_target="tpu_custom_call" | custom-call | tf_op jit(solution)/shard_map/pallas_call | solution.py:323
  59.3 0.6 %bitcast_divide_fusion = (f32[126,48]{0,1:T(8,128)}, f32[126,48]{0,1:T(8,128)}) fusion(f32[48,128]{1,0:T(8,128)S(1)} %get-tuple-element.5, f32[48,128]{1,0:T(8,128)S(1)} %get-tuple-element.4), kind=kLoop, calls=%fused_computation | loop fusion | flops 6048 | bytes 96768 | tf_op jit(solution)/shard_map/div | solution.py:351
